TPU v7x, 32 devices: a whole 2x2x4 slice. The times are simulated.
32 devices in a mesh: row: 16 (over z, x, core), col: 2 (over y).
Axes of the slice: x: 2, y: 2, z: 4, core: 2. Of those that a mesh axis runs over, the one named last changes fastest.
Arguments:
- activations: bfloat16 [128, 16384], P('col', 'row'), may hold values from 0 to 2
- blocks_one: bfloat16 [16, 2, 64, 128, 128], P('row', 'col'), may hold values from -0.25 to 0.25
- pattern_one: int32 [16, 2, 64], P('row', 'col'), may hold values from 0 to 511, as said below
- count_one: int32 [16, 2], P('row', 'col'), may hold values from 1 to 64, as said below
- blocks_two: bfloat16 [2, 16, 64, 128, 128], P('col', 'row'), may hold values from -0.375 to 0.375
- pattern_two: int32 [2, 16, 64], P('col', 'row'), may hold values from 0 to 511, as said below
- count_two: int32 [2, 16], P('col', 'row'), may hold values from 1 to 64, as said below
Outputs:
- sparse_out: bfloat16 [128, 16384], P('col', 'row')
Inputs may be any that keep to these rules, and one draw needn't show every extreme that they name: `pattern_one`: in each tile the slots below its count hold distinct positions; slots at or above the count hold positions in range whose blocks are not part of the weights. `count_one`: some tile has exactly 64 live slots. `pattern_two`: in each tile the slots below its count hold distinct positions; slots at or above the count hold positions in range whose blocks are not part of the weights. `count_two`: some tile has exactly 64 live slots.
All inputs are finite; a program needn't handle non-finite values.
Results may differ from a plain program's by a relative error of at most 0.0053.
Values may be sent and summed in bfloat16 or wider, within the bound.
No kernel may reach another device: no remote copies, remote signals or barrier semaphores. Data moves between devices by JAX's collectives and lax.ppermute only.
A program may use at most 64 MiB of HBM per device.

v0:
```python
import functools
import math

import jax
import jax.numpy as jnp
from jax import lax
from jax.experimental import pallas as pl
from jax.experimental.pallas import tpu as pltpu
from jax.sharding import PartitionSpec as P


bias_value = -0.3
CORES = 2
DEPTH = 4
STEP_BYTES = 2 * 1024 * 1024
SEND = jnp.float32
SPARE = 1024 * 1024
PLANS = 2
CUTS = 2


def slots_a_step(slots, rows, size):
    step = slots
    while step > 8 and step * rows * size * 4 > STEP_BYTES:
        step //= 2
    return step


def split(value, by):
    if by & (by - 1) == 0:
        return lax.shift_right_logical(value, by.bit_length() - 1), value & (by - 1)
    return value // by, value % by


def turned(digit, by, size):
    if size & (size - 1) == 0:
        return digit ^ by
    return (digit + by) % size


def sender(digit, by, size):
    if size & (size - 1) == 0:
        return digit ^ by
    return (digit + size - by) % size


def digit_shift(sizes, which, by):
    total = sizes[0] * sizes[1] * sizes[2]
    stride = 1
    for size in sizes[which + 1 :]:
        stride *= size
    size = sizes[which]
    pairs = []
    for r in range(total):
        d = (r // stride) % size
        pairs.append((r, r + (turned(d, by, size) - d) * stride))
    return pairs


def first_kernel(sizes, groups, load, *refs):
    _, width, cores = sizes
    if load:
        count, plans, (act, blocks), refs = refs[0], refs[1 : 1 + PLANS], refs[1 + PLANS : 3 + PLANS], refs[3 + PLANS :]
        held, *here, stage, acc, sems = refs[2 * width :]
        slots, size, _ = blocks.shape
        moves = [(plan, there) for plan, there in zip(plans, here)]
        moves += [(act.at[:, pl.ds(r * size, size)], stage.at[r]) for r in range(stage.shape[0])]
        moves.append((blocks, held))
        copies = [pltpu.make_async_copy(a, b, sems.at[i]) for i, (a, b) in enumerate(moves)]
        for copy in copies:
            copy.start()
        for copy in copies[:PLANS]:
            copy.wait()
        copies = copies[PLANS:]
        blocks = held
        pattern = here[0]
    else:
        pattern, count, act, blocks = refs[:4]
        refs = refs[4:]
        slots, size, _ = blocks.shape
        stage, acc = refs[2 * width :]
    units, m, _ = acc.shape
    units -= groups
    columns = units // groups
    unroll = slots_a_step(slots, m * groups, size)
    live = count[0, 0]
    if not load:
        for r in range(stage.shape[0]):
            stage[r] = act[:, r * size : (r + 1) * size]

    def clear(u, _):
        acc[u] = jnp.zeros((m, size), jnp.float32)
        return 0

    lax.fori_loop(0, units, clear, 0, unroll=8)
    if load:
        for copy in copies:
            copy.wait()

    def step(t, _):
        base = t * unroll
        found = []
        for j in range(unroll):
            r, c = split(pattern[0, base + j], columns)
            product = jnp.dot(stage[r], blocks[base + j], preferred_element_type=jnp.float32)
            found.append((c, product))
        for j, (c, product) in enumerate(found):
            used = base + j < live
            for g in range(groups):
                at = jnp.where(used, g * columns + c, units + g)
                acc[at] += product[g * m : (g + 1) * m]
        return 0

    lax.fori_loop(0, (live + unroll - 1) // unroll, step, 0)
    row = lax.axis_index("row")
    core, x = row % cores, row // cores % width
    per = units // (cores * width)
    for k in range(width):
        xd = turned(x, k, width)
        mine = (core * width + xd) * per
        other = ((cores - 1 - core) * width + xd) * per
        send, keep = refs[k], refs[width + k]

        def leave(u, _):
            send[u] = acc[other + u].astype(send.dtype)
            keep[u] = acc[mine + u]
            return 0

        lax.fori_loop(0, per, leave, 0, unroll=4)


def pair_kernel(left, right, out):
    def step(j, _):
        out[j] = (left[j] + right[j].astype(jnp.float32)).astype(out.dtype)
        return 0

    lax.fori_loop(0, out.shape[0], step, 0, unroll=4)


def spread_kernel(size, stride, *refs):
    arrays, outs = refs[:-size], refs[-size:]
    here = lax.axis_index("row") // stride % size

    def step(j, _):
        for k, out in enumerate(outs):
            at = turned(here, k, size)
            total = arrays[0][at, j]
            for a in arrays[1:]:
                total = total + a[at, j].astype(jnp.float32)
            out[j] = total.astype(out.dtype)
        return 0

    lax.fori_loop(0, outs[0].shape[0], step, 0, unroll=2)


def finish_kernel(*refs):
    def step(j, _):
        total = refs[0][j]
        for a in refs[1:-1]:
            total = total + a[j].astype(jnp.float32)
        refs[-1][j] = jnp.maximum(total + bias_value, 0.0).astype(jnp.bfloat16)
        return 0

    lax.fori_loop(0, refs[0].shape[0], step, 0, unroll=True if refs[0].shape[0] < 8 else 4)


def join_kernel(cuts, *refs):
    arrays, outs = refs[:-cuts], refs[-cuts:]
    n = arrays[0].shape[0]
    m = outs[0].shape[1]
    for h, out in enumerate(outs):
        for i, ref in enumerate(arrays):
            for j in range(n):
                out[i * n + j] = ref[j, h * m : (h + 1) * m]


def second_kernel(sizes, groups, pattern, count, *refs):
    depth, width, cores = sizes
    pieces = refs[: width * cores]
    blocks, out, hidden, acc = refs[width * cores :]
    slots, size, _ = blocks.shape
    units, m, _ = hidden.shape
    columns = acc.shape[0] - 1
    rows_in = units // groups
    unroll = slots_a_step(slots, m * groups, size)
    each = units // (depth * width * cores)
    live = count[0, 0]
    row = lax.axis_index("row")
    core, x, z = row % cores, row // cores % width, row // (cores * width)
    for c in range(columns):
        acc[c] = jnp.zeros(acc.shape[1:], jnp.float32)
    for i, piece in enumerate(pieces):
        cd, xd = sender(core, i // width, cores), sender(x, i % width, width)
        for k in range(depth):
            base = ((cd * width + xd) * depth + sender(z, k, depth)) * each
            for j in range(each):
                hidden[base + j] = piece[k * each + j]

    def step(t, _):
        base = t * unroll
        found = []
        for j in range(unroll):
            block = blocks[base + j]
            r, c = split(pattern[0, base + j], columns)
            products = [
                jnp.dot(hidden[g * rows_in + r], block, preferred_element_type=jnp.float32) for g in range(groups)
            ]
            found.append((c, products))
        for j, (c, products) in enumerate(found):
            at = jnp.where(base + j < live, c, columns)
            for g, product in enumerate(products):
                acc[at, g * m : (g + 1) * m] += product
        return 0

    lax.fori_loop(0, (live + unroll - 1) // unroll, step, 0)
    for c in range(columns):
        out[:, c * size : (c + 1) * size] = acc[c].astype(out.dtype)


def shards(sizes, n_cols, activations, blocks_one, pattern_one, count_one, blocks_two, pattern_two, count_two):
    depth, width, cores = sizes
    n_rows = depth * width * cores
    own_rows, features = activations.shape
    slots, size = blocks_one.shape[2], blocks_one.shape[3]
    columns_one = features * n_rows // n_cols // size
    columns_two = features // size
    groups = max(1, n_rows // columns_one)
    cuts = CUTS if n_cols == 2 and groups == 1 else 1
    units = columns_one * groups
    per = units // (width * cores)
    each = per // depth
    smem = pl.BlockSpec(memory_space=pltpu.SMEM)
    vmem = pl.BlockSpec(memory_space=pltpu.VMEM)
    anyspace = pl.BlockSpec(memory_space=pl.ANY)

    def move(value, which, by):
        return lax.ppermute(value, "row", digit_shift(sizes, which, by))

    def across(value, by):
        return lax.ppermute(value, "col", [(b, (b + by) % n_cols) for b in range(n_cols)])

    def call(kernel, outs, scalars, arrays, scratch=(), rows=0, copies=0, tables=0):
        total = sum(math.prod(a.shape) * a.dtype.itemsize for a in (*arrays, *outs, *scratch))
        cost = None
        if rows:
            cost = pl.CostEstimate(
                flops=2 * slots * rows * size * size, bytes_accessed=slots * size * size * 2, transcendentals=0
            )
        return pl.pallas_call(
            kernel,
            out_shape=tuple(outs),
            in_specs=[smem] * len(scalars) + [anyspace if copies else vmem] * len(arrays),
            out_specs=(vmem,) * (len(outs) - tables) + (smem,) * tables,
            scratch_shapes=[pltpu.VMEM(a.shape, a.dtype) for a in scratch]
            + [pltpu.SemaphoreType.DMA((copies,))] * bool(copies),
            compiler_params=pltpu.CompilerParams(vmem_limit_bytes=total + SPARE),
            cost_estimate=cost,
        )(*scalars, *arrays)

    def first(act, plans, stored=None):
        load = stored is None
        rows = act.shape[0]
        m = rows // groups
        shape = (per, m, size)
        outs = [jax.ShapeDtypeStruct(shape, kind) for kind in (SEND, jnp.float32) for _ in range(width)]
        scratch = [
            jax.ShapeDtypeStruct((columns_two, rows, size), jnp.bfloat16),
            jax.ShapeDtypeStruct((units + groups, m, size), jnp.float32),
        ]
        kernel = functools.partial(first_kernel, sizes, groups, load)
        if not load:
            return call(kernel, outs, [plans[0], count_one], [act, stored], scratch, rows)
        arrays = [*plans, act, blocks_one.reshape(slots, size, size)]
        arrays = [pltpu.with_memory_space_constraint(a, pltpu.HBM) for a in arrays]
        outs.append(jax.ShapeDtypeStruct(arrays[-1].shape, jnp.bfloat16))
        outs += [pltpu.SMEM(p.shape, p.dtype) for p in plans]
        return call(kernel, outs, [count_one], arrays, scratch, rows, columns_two + 1 + PLANS, PLANS)

    def reduce_core(arrays):
        steps = [*range(1, width), 0]
        got = {}
        for k in steps:
            got[k] = move(arrays[k], 2, 1)
        return [(arrays[width + k], got[k]) for k in range(width)]

    def reduce_width(pairs):
        gets = []
        for k in range(1, width):
            out = jax.ShapeDtypeStruct(pairs[k][0].shape, jnp.bfloat16)
            gets.append(move(call(pair_kernel, [out], [], pairs[k])[0], 1, k))
        return [*pairs[0], *gets]

    def reduce_depth(arrays):
        arrays = [a.reshape((depth, each) + a.shape[1:]) for a in arrays]
        kinds = [jnp.float32] + [jnp.bfloat16] * (depth - 1)
        outs = [jax.ShapeDtypeStruct(arrays[0].shape[1:], kind) for kind in kinds]
        outs = call(functools.partial(spread_kernel, depth, width * cores), outs, [], arrays)
        arrays = [outs[0]] + [move(out, 0, k + 1) for k, out in enumerate(outs[1:])]
        return call(finish_kernel, [jax.ShapeDtypeStruct(arrays[0].shape, jnp.bfloat16)], [], arrays)[0]

    def gather_depth(hidden, cuts):
        arrays = [hidden] + [move(hidden, 0, k) for k in range(1, depth)]
        joined = (depth * each, hidden.shape[1] // cuts, hidden.shape[2])
        outs = [jax.ShapeDtypeStruct(joined, jnp.bfloat16)] * cuts
        return call(functools.partial(join_kernel, cuts), outs, [], arrays)

    def gather_width(line):
        far = [move(line, 1, k) for k in range(1, width)]
        near = [move(line, 2, k) for k in range(1, cores)]
        return [line, *far] + [p for k in range(1, cores) for p in (near[k - 1], *(move(f, 2, k) for f in far))]

    def second(pieces, plans, out_type):
        rows = pieces[0].shape[1] * groups
        return call(
            functools.partial(second_kernel, sizes, groups),
            [jax.ShapeDtypeStruct((rows, features), out_type)],
            [plans[1], count_two],
            [*pieces, blocks_two.reshape(slots, size, size)],
            [
                jax.ShapeDtypeStruct((units, rows // groups, size), jnp.bfloat16),
                jax.ShapeDtypeStruct((columns_two + 1, rows, size), jnp.float32),
            ],
            rows if out_type == jnp.bfloat16 else 0,
        )[0]

    theirs = [across(activations, k) for k in range(1, n_cols)]
    theirs = theirs[0] if n_cols == 2 else jnp.concatenate(theirs, axis=0)
    plans = [pattern_one.reshape(1, slots), pattern_two.reshape(1, slots)]
    *own, stored, plan_one, plan_two = first(activations, plans)
    plans = [plan_one, plan_two]
    theirs = first(theirs, plans, stored)
    chunks = {"theirs": theirs, "own": own}
    stages = {
        "reduce_core": reduce_core,
        "reduce_width": reduce_width,
        "reduce_depth": reduce_depth,
    }
    for run in stages.values():
        for name in chunks:
            chunks[name] = run(chunks[name])
    lines = gather_depth(chunks["theirs"], cuts)
    own_line = gather_depth(chunks["own"], 1)[0]
    rest = []
    for line in lines:
        pieces = gather_width(line)
        rest.append(second(pieces, plans, jnp.bfloat16))
    pieces = gather_width(own_line)
    mine = second(pieces, plans, jnp.float32)
    for k in range(1, n_cols):
        back = []
        for part in rest:
            rows = own_rows if cuts == 1 else part.shape[0]
            back.append(across(lax.slice_in_dim(part, (k - 1) * rows, k * rows, axis=0), -k))
        back = back[0] if cuts == 1 else jnp.concatenate(back, axis=0)
        mine = mine + back.astype(jnp.float32)
    return jnp.maximum(mine + bias_value, 0.0).astype(jnp.bfloat16)


def solution(mesh):
    n_rows, n_cols = mesh.shape["row"], mesh.shape["col"]
    sizes = (DEPTH, n_rows // (DEPTH * CORES), CORES)
    in_specs = (
        P("col", "row"),
        P("row", "col", None, None, None),
        P("row", "col", None),
        P("row", "col"),
        P("col", "row", None, None, None),
        P("col", "row", None),
        P("col", "row"),
    )
    return jax.shard_map(
        functools.partial(shards, sizes, n_cols),
        mesh=mesh,
        in_specs=in_specs,
        out_specs=P("col", "row"),
        check_vma=False,
    )
```

profile of v0, /device:TPU:0, one launch (start us, length us, event | category | flops | bytes accessed | tf_op | source)
XLA Modules:
  0.0 76.7 jit_solution(5980626821210446544)
XLA Ops:
  0.7 2.7 %shard_map.73 = (f32[16,64,128]{2,1,0:T(8,128)S(1)}, f32[16,64,128]{2,1,0:T(8,128)S(1)}, f32[16,64,128]{2,1,0:T(8,128)S(1)}, f32[16,64,128]{2,1,0:T(8,128)S(1)},...) custom-call(s32[1,1]{1,0:T(1,128)S(6)} %copy.8.refs_0_.refs_1_, s32[1,64]{1,0:T(1,128)} %bitcast.20, ...), custom_call_target="tpu_custom_call" | custom-call | flops 134217728 | bytes 2097152 | tf_op jit(solution)/shard_map/pallas_call | solution.py:249
  4.0 2.6 %collective-permute-start.12 = (bf16[64,1024]{1,0:T(8,128)(2,1)S(1)}, bf16[64,1024]{1,0:T(8,128)(2,1)S(1)}, u32[]{:S(2)}, u32[]{:S(2)}) collective-permute-start(bf16[64,1024]{1,0:T(8,128)(2,1)S(1)} %copy-done.1), channel_id=1, source_target_pairs={{0,1},{1,0},{2,3},{3,2},{4,5},{5,4},{6,7},{7,6},{8,9},{9,8},{10,11... | collective-permute-start | bytes 393224 | tf_op jit(solution)/shard_map/ppermute | solution.py:240
  6.6 4.1 %collective-permute-done.12.refs_2_ = bf16[64,1024]{1,0:T(8,128)(2,1)S(1)} collective-permute-done((bf16[64,1024]{1,0:T(8,128)(2,1)S(1)}, bf16[64,1024]{1,0:T(8,128)(2,1)S(1)}, u32[]{:S(2)}, u32[]{:S(2)}) %collective-permute-start.12) | collective-permute-done | bytes 131104 | tf_op jit(solution)/shard_map/ppermute | solution.py:240
  10.7 1.1 %shard_map.79 = (f32[16,64,128]{2,1,0:T(8,128)S(1)}, f32[16,64,128]{2,1,0:T(8,128)S(1)}, f32[16,64,128]{2,1,0:T(8,128)S(1)}, f32[16,64,128]{2,1,0:T(8,128)S(1)}) custom-call(s32[1,64]{1,0:T(1,128)S(4)} %get-tuple-element.35.refs_0_, s32[1,1]{1,0:T(1,128)S(6)} %copy.8.refs_0_.refs_1_, bf16[64,1024]{1,0:T(8,128)(2,1)S(1)} %collective-permute-done.12.refs_2_, ...), custom_call_target="tpu_custom_call" | custom-call | flops 134217728 | bytes 2097152 | tf_op jit(solution)/shard_map/pallas_call | solution.py:249
  12.5 1.8 %collective-permute-start.2 = (bf16[16,64,128]{2,1,0:T(8,128)(2,1)S(1)}, bf16[16,64,128]{2,1,0:T(8,128)(2,1)S(1)}, u32[]{:S(2)}, u32[]{:S(2)}) collective-permute-start(bf16[16,64,128]{2,1,0:T(8,128)(2,1)S(1)} %shard_map.74), channel_id=1, source_target_pairs={{0,4},{2,6},{4,0},{6,2},{8,12},{10,14},{12,8},{14,10},{16,20},{18,... | collective-permute-start | bytes 786440 | tf_op jit(solution)/shard_map/ppermute | solution.py:237
  14.3 1.2 %collective-permute-start.15 = (bf16[16,64,128]{2,1,0:T(8,128)(2,1)S(1)}, bf16[16,64,128]{2,1,0:T(8,128)(2,1)S(1)}, u32[]{:S(2)}, u32[]{:S(2)}) collective-permute-start(bf16[16,64,128]{2,1,0:T(8,128)(2,1)S(1)} %shard_map.80), channel_id=1, source_target_pairs={{0,4},{2,6},{4,0},{6,2},{8,12},{10,14},{12,8},{14,10},{16,20},{18,... | collective-permute-start | bytes 786440 | tf_op jit(solution)/shard_map/ppermute | solution.py:237
  15.5 6.2 %collective-permute-done.2 = bf16[16,64,128]{2,1,0:T(8,128)(2,1)S(1)} collective-permute-done((bf16[16,64,128]{2,1,0:T(8,128)(2,1)S(1)}, bf16[16,64,128]{2,1,0:T(8,128)(2,1)S(1)}, u32[]{:S(2)}, u32[]{:S(2)}) %collective-permute-start.2) | collective-permute-done | bytes 262176 | tf_op jit(solution)/shard_map/ppermute | solution.py:237
  21.8 1.8 %collective-permute-start.3 = (bf16[4,64,128]{2,1,0:T(8,128)(2,1)S(1)}, bf16[4,64,128]{2,1,0:T(8,128)(2,1)S(1)}, u32[]{:S(2)}, u32[]{:S(2)}) collective-permute-start(bf16[4,64,128]{2,1,0:T(8,128)(2,1)S(1)} %get-tuple-element.32), channel_id=1, source_target_pairs={{0,8},{2,10},{4,12},{6,14},{8,0},{10,2},{12,4},{14,6},{16,24},{18,... | collective-permute-start | bytes 196616 | tf_op jit(solution)/shard_map/ppermute | solution.py:237
  23.7 2.6 %collective-permute-start.4 = (bf16[4,64,128]{2,1,0:T(8,128)(2,1)S(1)}, bf16[4,64,128]{2,1,0:T(8,128)(2,1)S(1)}, u32[]{:S(2)}, u32[]{:S(2)}) collective-permute-start(bf16[4,64,128]{2,1,0:T(8,128)(2,1)S(1)} %get-tuple-element.33), channel_id=1, source_target_pairs={{0,16},{2,18},{4,20},{6,22},{8,24},{10,26},{12,28},{14,30},{16,0},... | collective-permute-start | bytes 196616 | tf_op jit(solution)/shard_map/ppermute | solution.py:237
  26.8 3.5 %collective-permute-done.4.refs_2_ = bf16[4,64,128]{2,1,0:T(8,128)(2,1)S(1)} collective-permute-done((bf16[4,64,128]{2,1,0:T(8,128)(2,1)S(1)}, bf16[4,64,128]{2,1,0:T(8,128)(2,1)S(1)}, u32[]{:S(2)}, u32[]{:S(2)}) %collective-permute-start.4) | collective-permute-done | bytes 65568 | tf_op jit(solution)/shard_map/ppermute | solution.py:237
  30.2 2.4 %collective-permute-done.5.refs_3_ = bf16[4,64,128]{2,1,0:T(8,128)(2,1)S(1)} collective-permute-done((bf16[4,64,128]{2,1,0:T(8,128)(2,1)S(1)}, bf16[4,64,128]{2,1,0:T(8,128)(2,1)S(1)}, u32[]{:S(2)}, u32[]{:S(2)}) %collective-permute-start.5) | collective-permute-done | bytes 65568 | tf_op jit(solution)/shard_map/ppermute | solution.py:237
  32.8 1.2 %collective-permute-start.7 = (bf16[4,64,128]{2,1,0:T(8,128)(2,1)S(1)}, bf16[4,64,128]{2,1,0:T(8,128)(2,1)S(1)}, u32[]{:S(2)}, u32[]{:S(2)}) collective-permute-start(bf16[4,64,128]{2,1,0:T(8,128)(2,1)S(1)} %shard_map.76.refs_0_), channel_id=1, source_target_pairs={{0,16},{2,18},{4,20},{6,22},{8,24},{10,26},{12,28},{14,30},{16,0},... | collective-permute-start | bytes 196616 | tf_op jit(solution)/shard_map/ppermute | solution.py:237
  34.0 3.2 %collective-permute-start.8 = (bf16[4,64,128]{2,1,0:T(8,128)(2,1)S(1)}, bf16[4,64,128]{2,1,0:T(8,128)(2,1)S(1)}, u32[]{:S(2)}, u32[]{:S(2)}) collective-permute-start(bf16[4,64,128]{2,1,0:T(8,128)(2,1)S(1)} %shard_map.76.refs_0_), channel_id=1, source_target_pairs={{0,24},{2,26},{4,28},{6,30},{8,16},{10,18},{12,20},{14,22},{16,8},... | collective-permute-start | bytes 196616 | tf_op jit(solution)/shard_map/ppermute | solution.py:237
  37.2 0.9 %collective-permute-done.7.refs_2_ = bf16[4,64,128]{2,1,0:T(8,128)(2,1)S(1)} collective-permute-done((bf16[4,64,128]{2,1,0:T(8,128)(2,1)S(1)}, bf16[4,64,128]{2,1,0:T(8,128)(2,1)S(1)}, u32[]{:S(2)}, u32[]{:S(2)}) %collective-permute-start.7) | collective-permute-done | bytes 65568 | tf_op jit(solution)/shard_map/ppermute | solution.py:237
  38.0 2.2 %collective-permute-done.8.refs_3_ = bf16[4,64,128]{2,1,0:T(8,128)(2,1)S(1)} collective-permute-done((bf16[4,64,128]{2,1,0:T(8,128)(2,1)S(1)}, bf16[4,64,128]{2,1,0:T(8,128)(2,1)S(1)}, u32[]{:S(2)}, u32[]{:S(2)}) %collective-permute-start.8) | collective-permute-done | bytes 65568 | tf_op jit(solution)/shard_map/ppermute | solution.py:237
  40.2 1.6 %collective-permute-start.9 = (bf16[16,64,128]{2,1,0:T(8,128)(2,1)S(1)}, bf16[16,64,128]{2,1,0:T(8,128)(2,1)S(1)}, u32[]{:S(2)}, u32[]{:S(2)}) collective-permute-start(bf16[16,64,128]{2,1,0:T(8,128)(2,1)S(1)} %shard_map.77.refs_0_), channel_id=1, source_target_pairs={{0,4},{2,6},{4,0},{6,2},{8,12},{10,14},{12,8},{14,10},{16,20},{18,... | collective-permute-start | bytes 786440 | tf_op jit(solution)/shard_map/ppermute | solution.py:237
  42.7 2.9 %collective-permute-start.17 = (bf16[4,64,128]{2,1,0:T(8,128)(2,1)S(1)}, bf16[4,64,128]{2,1,0:T(8,128)(2,1)S(1)}, u32[]{:S(2)}, u32[]{:S(2)}) collective-permute-start(bf16[4,64,128]{2,1,0:T(8,128)(2,1)S(1)} %get-tuple-element.43), channel_id=1, source_target_pairs={{0,16},{2,18},{4,20},{6,22},{8,24},{10,26},{12,28},{14,30},{16,0},... | collective-permute-start | bytes 196616 | tf_op jit(solution)/shard_map/ppermute | solution.py:237
  45.5 0.8 %collective-permute-start.18 = (bf16[4,64,128]{2,1,0:T(8,128)(2,1)S(1)}, bf16[4,64,128]{2,1,0:T(8,128)(2,1)S(1)}, u32[]{:S(2)}, u32[]{:S(2)}) collective-permute-start(bf16[4,64,128]{2,1,0:T(8,128)(2,1)S(1)} %get-tuple-element.44), channel_id=1, source_target_pairs={{0,24},{2,26},{4,28},{6,30},{8,16},{10,18},{12,20},{14,22},{16,8},... | collective-permute-start | bytes 196616 | tf_op jit(solution)/shard_map/ppermute | solution.py:237
  46.5 1.4 %collective-permute-done.17.refs_2_ = bf16[4,64,128]{2,1,0:T(8,128)(2,1)S(1)} collective-permute-done((bf16[4,64,128]{2,1,0:T(8,128)(2,1)S(1)}, bf16[4,64,128]{2,1,0:T(8,128)(2,1)S(1)}, u32[]{:S(2)}, u32[]{:S(2)}) %collective-permute-start.17) | collective-permute-done | bytes 65568 | tf_op jit(solution)/shard_map/ppermute | solution.py:237
  47.9 4.5 %collective-permute-done.18.refs_3_ = bf16[4,64,128]{2,1,0:T(8,128)(2,1)S(1)} collective-permute-done((bf16[4,64,128]{2,1,0:T(8,128)(2,1)S(1)}, bf16[4,64,128]{2,1,0:T(8,128)(2,1)S(1)}, u32[]{:S(2)}, u32[]{:S(2)}) %collective-permute-start.18) | collective-permute-done | bytes 65568 | tf_op jit(solution)/shard_map/ppermute | solution.py:237
  52.5 1.5 %collective-permute-start.20 = (bf16[4,64,128]{2,1,0:T(8,128)(2,1)S(1)}, bf16[4,64,128]{2,1,0:T(8,128)(2,1)S(1)}, u32[]{:S(2)}, u32[]{:S(2)}) collective-permute-start(bf16[4,64,128]{2,1,0:T(8,128)(2,1)S(1)} %shard_map.82.refs_0_), channel_id=1, source_target_pairs={{0,16},{2,18},{4,20},{6,22},{8,24},{10,26},{12,28},{14,30},{16,0},... | collective-permute-start | bytes 196616 | tf_op jit(solution)/shard_map/ppermute | solution.py:237
  54.0 2.9 %collective-permute-start.21 = (bf16[4,64,128]{2,1,0:T(8,128)(2,1)S(1)}, bf16[4,64,128]{2,1,0:T(8,128)(2,1)S(1)}, u32[]{:S(2)}, u32[]{:S(2)}) collective-permute-start(bf16[4,64,128]{2,1,0:T(8,128)(2,1)S(1)} %shard_map.82.refs_0_), channel_id=1, source_target_pairs={{0,24},{2,26},{4,28},{6,30},{8,16},{10,18},{12,20},{14,22},{16,8},... | collective-permute-start | bytes 196616 | tf_op jit(solution)/shard_map/ppermute | solution.py:237
  56.9 0.9 %collective-permute-done.20.refs_2_ = bf16[4,64,128]{2,1,0:T(8,128)(2,1)S(1)} collective-permute-done((bf16[4,64,128]{2,1,0:T(8,128)(2,1)S(1)}, bf16[4,64,128]{2,1,0:T(8,128)(2,1)S(1)}, u32[]{:S(2)}, u32[]{:S(2)}) %collective-permute-start.20) | collective-permute-done | bytes 65568 | tf_op jit(solution)/shard_map/ppermute | solution.py:237
  57.8 2.4 %collective-permute-done.21.refs_3_ = bf16[4,64,128]{2,1,0:T(8,128)(2,1)S(1)} collective-permute-done((bf16[4,64,128]{2,1,0:T(8,128)(2,1)S(1)}, bf16[4,64,128]{2,1,0:T(8,128)(2,1)S(1)}, u32[]{:S(2)}, u32[]{:S(2)}) %collective-permute-start.21) | collective-permute-done | bytes 65568 | tf_op jit(solution)/shard_map/ppermute | solution.py:237
  60.1 0.8 %collective-permute-start.26 = (bf16[16,32,128]{2,1,0:T(8,128)(2,1)S(1)}, bf16[16,32,128]{2,1,0:T(8,128)(2,1)S(1)}, u32[]{:S(2)}, u32[]{:S(2)}) collective-permute-start(bf16[16,32,128]{2,1,0:T(8,128)(2,1)S(1)} %get-tuple-element.46.refs_0_), channel_id=1, source_target_pairs={{0,4},{2,6},{4,0},{6,2},{8,12},{10,14},{12,8},{14,10},{16,20},{18,... | collective-permute-start | bytes 393224 | tf_op jit(solution)/shard_map/ppermute | solution.py:237
  60.9 1.3 %collective-permute-start.22 = (bf16[16,32,128]{2,1,0:T(8,128)(2,1)S(1)}, bf16[16,32,128]{2,1,0:T(8,128)(2,1)S(1)}, u32[]{:S(2)}, u32[]{:S(2)}) collective-permute-start(bf16[16,32,128]{2,1,0:T(8,128)(2,1)S(1)} %get-tuple-element.45.refs_0_), channel_id=1, source_target_pairs={{0,4},{2,6},{4,0},{6,2},{8,12},{10,14},{12,8},{14,10},{16,20},{18,... | collective-permute-start | bytes 393224 | tf_op jit(solution)/shard_map/ppermute | solution.py:237
  62.7 3.5 %collective-permute-done.26.refs_1_ = bf16[16,32,128]{2,1,0:T(8,128)(2,1)S(1)} collective-permute-done((bf16[16,32,128]{2,1,0:T(8,128)(2,1)S(1)}, bf16[16,32,128]{2,1,0:T(8,128)(2,1)S(1)}, u32[]{:S(2)}, u32[]{:S(2)}) %collective-permute-start.26) | collective-permute-done | bytes 131104 | tf_op jit(solution)/shard_map/ppermute | solution.py:237
  66.8 1.2 %collective-permute-done.22.refs_1_ = bf16[16,32,128]{2,1,0:T(8,128)(2,1)S(1)} collective-permute-done((bf16[16,32,128]{2,1,0:T(8,128)(2,1)S(1)}, bf16[16,32,128]{2,1,0:T(8,128)(2,1)S(1)}, u32[]{:S(2)}, u32[]{:S(2)}) %collective-permute-start.22) | collective-permute-done | bytes 131104 | tf_op jit(solution)/shard_map/ppermute | solution.py:237
  68.6 0.8 %shard_map.85 = bf16[32,1024]{1,0:T(8,128)(2,1)S(1)} custom-call(s32[1,64]{1,0:T(1,128)S(4)} %get-tuple-element.26.pattern, s32[1,1]{1,0:T(1,128)S(6)} %copy.9.count, bf16[16,32,128]{2,1,0:T(8,128)(2,1)S(1)} %get-tuple-element.46.refs_0_, bf16[16,32,128]{2,1,0:T(8,128)(2,1)S(1)} %collective-permute-done.26.refs_1_, ...), custom_call_target="tpu_custom_call" | custom-call | flops 67108864 | bytes 2097152 | tf_op jit(solution)/shard_map/pallas_call | solution.py:249
  69.4 1.5 %collective-permute-start.29 = (bf16[32,1024]{1,0:T(8,128)(2,1)S(1)}, bf16[32,1024]{1,0:T(8,128)(2,1)S(1)}, u32[]{:S(2)}, u32[]{:S(2)}) collective-permute-start(bf16[32,1024]{1,0:T(8,128)(2,1)S(1)} %shard_map.85), channel_id=1, source_target_pairs={{0,1},{1,0},{2,3},{3,2},{4,5},{5,4},{6,7},{7,6},{8,9},{9,8},{10,11... | collective-permute-start | bytes 196616 | tf_op jit(solution)/shard_map/ppermute | solution.py:240
  72.4 0.9 %shard_map.78 = f32[64,1024]{1,0:T(8,128)S(1)} custom-call(s32[1,64]{1,0:T(1,128)S(4)} %get-tuple-element.26.pattern, s32[1,1]{1,0:T(1,128)S(6)} %copy.9.count, bf16[16,64,128]{2,1,0:T(8,128)(2,1)S(1)} %shard_map.77.refs_0_, bf16[16,64,128]{2,1,0:T(8,128)(2,1)S(1)} %collective-permute-done.9.refs_1_, ...), custom_call_target="tpu_custom_call" | custom-call | tf_op jit(solution)/shard_map/pallas_call | solution.py:249
  74.0 2.1 %collective-permute-done.25 = bf16[32,1024]{1,0:T(8,128)(2,1)S(1)} collective-permute-done((bf16[32,1024]{1,0:T(8,128)(2,1)S(1)}, bf16[32,1024]{1,0:T(8,128)(2,1)S(1)}, u32[]{:S(2)}, u32[]{:S(2)}) %collective-permute-start.25) | collective-permute-done | bytes 65568 | tf_op jit(solution)/shard_map/ppermute | solution.py:240
  (46 shorter events, 7.2 us)
Async XLA Ops:
  0.0 4.0 %copy-start.1 = (bf16[64,1024]{1,0:T(8,128)(2,1)S(1)}, bf16[64,1024]{1,0:T(8,128)(2,1)}, u32[]{:S(2)}) copy-start(bf16[64,1024]{1,0:T(8,128)(2,1)} %refs_3_.1) | copy-start | bytes 393220
  3.4 9.0 %collective-permute-start.1 = (f32[16,64,128]{2,1,0:T(8,128)S(1)}, f32[16,64,128]{2,1,0:T(8,128)S(1)}, u32[]{:S(2)}, u32[]{:S(2)}) collective-permute-start(f32[16,64,128]{2,1,0:T(8,128)S(1)} %get-tuple-element.30), channel_id=1, source_target_pairs={{0,2},{2,0},{4,6},{6,4},{8,10},{10,8},{12,14},{14,12},{16,18},{18,... | collective-permute-start | bytes 1572872 | tf_op jit(solution)/shard_map/ppermute | solution.py:237
  4.0 6.7 %collective-permute-start.12 = (bf16[64,1024]{1,0:T(8,128)(2,1)S(1)}, bf16[64,1024]{1,0:T(8,128)(2,1)S(1)}, u32[]{:S(2)}, u32[]{:S(2)}) collective-permute-start(bf16[64,1024]{1,0:T(8,128)(2,1)S(1)} %copy-done.1), channel_id=1, source_target_pairs={{0,1},{1,0},{2,3},{3,2},{4,5},{5,4},{6,7},{7,6},{8,9},{9,8},{10,11... | collective-permute-start | bytes 393224 | tf_op jit(solution)/shard_map/ppermute | solution.py:240
  11.7 2.5 %collective-permute-start.14 = (f32[16,64,128]{2,1,0:T(8,128)S(1)}, f32[16,64,128]{2,1,0:T(8,128)S(1)}, u32[]{:S(2)}, u32[]{:S(2)}) collective-permute-start(f32[16,64,128]{2,1,0:T(8,128)S(1)} %get-tuple-element.40), channel_id=1, source_target_pairs={{0,2},{2,0},{4,6},{6,4},{8,10},{10,8},{12,14},{14,12},{16,18},{18,... | collective-permute-start | bytes 1572872 | tf_op jit(solution)/shard_map/ppermute | solution.py:237
  11.8 3.7 %collective-permute-start = (f32[16,64,128]{2,1,0:T(8,128)S(1)}, f32[16,64,128]{2,1,0:T(8,128)S(1)}, u32[]{:S(2)}, u32[]{:S(2)}) collective-permute-start(f32[16,64,128]{2,1,0:T(8,128)S(1)} %get-tuple-element.28), channel_id=1, source_target_pairs={{0,2},{2,0},{4,6},{6,4},{8,10},{10,8},{12,14},{14,12},{16,18},{18,... | collective-permute-start | bytes 1572872 | tf_op jit(solution)/shard_map/ppermute | solution.py:237
  12.3 29.5 %collective-permute-start.13 = (f32[16,64,128]{2,1,0:T(8,128)S(1)}, f32[16,64,128]{2,1,0:T(8,128)S(1)}, u32[]{:S(2)}, u32[]{:S(2)}) collective-permute-start(f32[16,64,128]{2,1,0:T(8,128)S(1)} %get-tuple-element.38), channel_id=1, source_target_pairs={{0,2},{2,0},{4,6},{6,4},{8,10},{10,8},{12,14},{14,12},{16,18},{18,... | collective-permute-start | bytes 1572872 | tf_op jit(solution)/shard_map/ppermute | solution.py:237
  12.5 9.2 %collective-permute-start.2 = (bf16[16,64,128]{2,1,0:T(8,128)(2,1)S(1)}, bf16[16,64,128]{2,1,0:T(8,128)(2,1)S(1)}, u32[]{:S(2)}, u32[]{:S(2)}) collective-permute-start(bf16[16,64,128]{2,1,0:T(8,128)(2,1)S(1)} %shard_map.74), channel_id=1, source_target_pairs={{0,4},{2,6},{4,0},{6,2},{8,12},{10,14},{12,8},{14,10},{16,20},{18,... | collective-permute-start | bytes 786440 | tf_op jit(solution)/shard_map/ppermute | solution.py:237
  14.3 27.5 %collective-permute-start.15 = (bf16[16,64,128]{2,1,0:T(8,128)(2,1)S(1)}, bf16[16,64,128]{2,1,0:T(8,128)(2,1)S(1)}, u32[]{:S(2)}, u32[]{:S(2)}) collective-permute-start(bf16[16,64,128]{2,1,0:T(8,128)(2,1)S(1)} %shard_map.80), channel_id=1, source_target_pairs={{0,4},{2,6},{4,0},{6,2},{8,12},{10,14},{12,8},{14,10},{16,20},{18,... | collective-permute-start | bytes 786440 | tf_op jit(solution)/shard_map/ppermute | solution.py:237
  21.7 46.9 %copy-start = (bf16[1,1,64,128,128]{4,3,2,1,0:T(8,128)(2,1)S(1)}, bf16[1,1,64,128,128]{4,3,2,1,0:T(8,128)(2,1)}, u32[]{:S(2)}) copy-start(bf16[1,1,64,128,128]{4,3,2,1,0:T(8,128)(2,1)} %param.11) | copy-start | bytes 6291460
  21.8 5.0 %collective-permute-start.3 = (bf16[4,64,128]{2,1,0:T(8,128)(2,1)S(1)}, bf16[4,64,128]{2,1,0:T(8,128)(2,1)S(1)}, u32[]{:S(2)}, u32[]{:S(2)}) collective-permute-start(bf16[4,64,128]{2,1,0:T(8,128)(2,1)S(1)} %get-tuple-element.32), channel_id=1, source_target_pairs={{0,8},{2,10},{4,12},{6,14},{8,0},{10,2},{12,4},{14,6},{16,24},{18,... | collective-permute-start | bytes 196616 | tf_op jit(solution)/shard_map/ppermute | solution.py:237
  23.7 6.6 %collective-permute-start.4 = (bf16[4,64,128]{2,1,0:T(8,128)(2,1)S(1)}, bf16[4,64,128]{2,1,0:T(8,128)(2,1)S(1)}, u32[]{:S(2)}, u32[]{:S(2)}) collective-permute-start(bf16[4,64,128]{2,1,0:T(8,128)(2,1)S(1)} %get-tuple-element.33), channel_id=1, source_target_pairs={{0,16},{2,18},{4,20},{6,22},{8,24},{10,26},{12,28},{14,30},{16,0},... | collective-permute-start | bytes 196616 | tf_op jit(solution)/shard_map/ppermute | solution.py:237
  26.3 6.4 %collective-permute-start.5 = (bf16[4,64,128]{2,1,0:T(8,128)(2,1)S(1)}, bf16[4,64,128]{2,1,0:T(8,128)(2,1)S(1)}, u32[]{:S(2)}, u32[]{:S(2)}) collective-permute-start(bf16[4,64,128]{2,1,0:T(8,128)(2,1)S(1)} %get-tuple-element.34), channel_id=1, source_target_pairs={{0,24},{2,26},{4,28},{6,30},{8,16},{10,18},{12,20},{14,22},{16,8},... | collective-permute-start | bytes 196616 | tf_op jit(solution)/shard_map/ppermute | solution.py:237
  32.7 4.5 %collective-permute-start.6 = (bf16[4,64,128]{2,1,0:T(8,128)(2,1)S(1)}, bf16[4,64,128]{2,1,0:T(8,128)(2,1)S(1)}, u32[]{:S(2)}, u32[]{:S(2)}) collective-permute-start(bf16[4,64,128]{2,1,0:T(8,128)(2,1)S(1)} %shard_map.76.refs_0_), channel_id=1, source_target_pairs={{0,8},{2,10},{4,12},{6,14},{8,0},{10,2},{12,4},{14,6},{16,24},{18,... | collective-permute-start | bytes 196616 | tf_op jit(solution)/shard_map/ppermute | solution.py:237
  32.8 5.2 %collective-permute-start.7 = (bf16[4,64,128]{2,1,0:T(8,128)(2,1)S(1)}, bf16[4,64,128]{2,1,0:T(8,128)(2,1)S(1)}, u32[]{:S(2)}, u32[]{:S(2)}) collective-permute-start(bf16[4,64,128]{2,1,0:T(8,128)(2,1)S(1)} %shard_map.76.refs_0_), channel_id=1, source_target_pairs={{0,16},{2,18},{4,20},{6,22},{8,24},{10,26},{12,28},{14,30},{16,0},... | collective-permute-start | bytes 196616 | tf_op jit(solution)/shard_map/ppermute | solution.py:237
  34.0 6.2 %collective-permute-start.8 = (bf16[4,64,128]{2,1,0:T(8,128)(2,1)S(1)}, bf16[4,64,128]{2,1,0:T(8,128)(2,1)S(1)}, u32[]{:S(2)}, u32[]{:S(2)}) collective-permute-start(bf16[4,64,128]{2,1,0:T(8,128)(2,1)S(1)} %shard_map.76.refs_0_), channel_id=1, source_target_pairs={{0,24},{2,26},{4,28},{6,30},{8,16},{10,18},{12,20},{14,22},{16,8},... | collective-permute-start | bytes 196616 | tf_op jit(solution)/shard_map/ppermute | solution.py:237
  40.2 22.2 %collective-permute-start.9 = (bf16[16,64,128]{2,1,0:T(8,128)(2,1)S(1)}, bf16[16,64,128]{2,1,0:T(8,128)(2,1)S(1)}, u32[]{:S(2)}, u32[]{:S(2)}) collective-permute-start(bf16[16,64,128]{2,1,0:T(8,128)(2,1)S(1)} %shard_map.77.refs_0_), channel_id=1, source_target_pairs={{0,4},{2,6},{4,0},{6,2},{8,12},{10,14},{12,8},{14,10},{16,20},{18,... | collective-permute-start | bytes 786440 | tf_op jit(solution)/shard_map/ppermute | solution.py:237
  41.9 4.6 %collective-permute-start.16 = (bf16[4,64,128]{2,1,0:T(8,128)(2,1)S(1)}, bf16[4,64,128]{2,1,0:T(8,128)(2,1)S(1)}, u32[]{:S(2)}, u32[]{:S(2)}) collective-permute-start(bf16[4,64,128]{2,1,0:T(8,128)(2,1)S(1)} %get-tuple-element.42), channel_id=1, source_target_pairs={{0,8},{2,10},{4,12},{6,14},{8,0},{10,2},{12,4},{14,6},{16,24},{18,... | collective-permute-start | bytes 196616 | tf_op jit(solution)/shard_map/ppermute | solution.py:237
  42.7 5.3 %collective-permute-start.17 = (bf16[4,64,128]{2,1,0:T(8,128)(2,1)S(1)}, bf16[4,64,128]{2,1,0:T(8,128)(2,1)S(1)}, u32[]{:S(2)}, u32[]{:S(2)}) collective-permute-start(bf16[4,64,128]{2,1,0:T(8,128)(2,1)S(1)} %get-tuple-element.43), channel_id=1, source_target_pairs={{0,16},{2,18},{4,20},{6,22},{8,24},{10,26},{12,28},{14,30},{16,0},... | collective-permute-start | bytes 196616 | tf_op jit(solution)/shard_map/ppermute | solution.py:237
  45.5 6.9 %collective-permute-start.18 = (bf16[4,64,128]{2,1,0:T(8,128)(2,1)S(1)}, bf16[4,64,128]{2,1,0:T(8,128)(2,1)S(1)}, u32[]{:S(2)}, u32[]{:S(2)}) collective-permute-start(bf16[4,64,128]{2,1,0:T(8,128)(2,1)S(1)} %get-tuple-element.44), channel_id=1, source_target_pairs={{0,24},{2,26},{4,28},{6,30},{8,16},{10,18},{12,20},{14,22},{16,8},... | collective-permute-start | bytes 196616 | tf_op jit(solution)/shard_map/ppermute | solution.py:237
  52.4 4.5 %collective-permute-start.19 = (bf16[4,64,128]{2,1,0:T(8,128)(2,1)S(1)}, bf16[4,64,128]{2,1,0:T(8,128)(2,1)S(1)}, u32[]{:S(2)}, u32[]{:S(2)}) collective-permute-start(bf16[4,64,128]{2,1,0:T(8,128)(2,1)S(1)} %shard_map.82.refs_0_), channel_id=1, source_target_pairs={{0,8},{2,10},{4,12},{6,14},{8,0},{10,2},{12,4},{14,6},{16,24},{18,... | collective-permute-start | bytes 196616 | tf_op jit(solution)/shard_map/ppermute | solution.py:237
  52.5 5.2 %collective-permute-start.20 = (bf16[4,64,128]{2,1,0:T(8,128)(2,1)S(1)}, bf16[4,64,128]{2,1,0:T(8,128)(2,1)S(1)}, u32[]{:S(2)}, u32[]{:S(2)}) collective-permute-start(bf16[4,64,128]{2,1,0:T(8,128)(2,1)S(1)} %shard_map.82.refs_0_), channel_id=1, source_target_pairs={{0,16},{2,18},{4,20},{6,22},{8,24},{10,26},{12,28},{14,30},{16,0},... | collective-permute-start | bytes 196616 | tf_op jit(solution)/shard_map/ppermute | solution.py:237
  54.0 6.1 %collective-permute-start.21 = (bf16[4,64,128]{2,1,0:T(8,128)(2,1)S(1)}, bf16[4,64,128]{2,1,0:T(8,128)(2,1)S(1)}, u32[]{:S(2)}, u32[]{:S(2)}) collective-permute-start(bf16[4,64,128]{2,1,0:T(8,128)(2,1)S(1)} %shard_map.82.refs_0_), channel_id=1, source_target_pairs={{0,24},{2,26},{4,28},{6,30},{8,16},{10,18},{12,20},{14,22},{16,8},... | collective-permute-start | bytes 196616 | tf_op jit(solution)/shard_map/ppermute | solution.py:237
  60.1 6.1 %collective-permute-start.26 = (bf16[16,32,128]{2,1,0:T(8,128)(2,1)S(1)}, bf16[16,32,128]{2,1,0:T(8,128)(2,1)S(1)}, u32[]{:S(2)}, u32[]{:S(2)}) collective-permute-start(bf16[16,32,128]{2,1,0:T(8,128)(2,1)S(1)} %get-tuple-element.46.refs_0_), channel_id=1, source_target_pairs={{0,4},{2,6},{4,0},{6,2},{8,12},{10,14},{12,8},{14,10},{16,20},{18,... | collective-permute-start | bytes 393224 | tf_op jit(solution)/shard_map/ppermute | solution.py:237
  60.9 5.3 %collective-permute-start.27 = (bf16[16,32,128]{2,1,0:T(8,128)(2,1)S(1)}, bf16[16,32,128]{2,1,0:T(8,128)(2,1)S(1)}, u32[]{:S(2)}, u32[]{:S(2)}) collective-permute-start(bf16[16,32,128]{2,1,0:T(8,128)(2,1)S(1)} %get-tuple-element.46.refs_0_), channel_id=1, source_target_pairs={{0,2},{2,0},{4,6},{6,4},{8,10},{10,8},{12,14},{14,12},{16,18},{18,... | collective-permute-start | bytes 393224 | tf_op jit(solution)/shard_map/ppermute | solution.py:237
  60.9 7.0 %collective-permute-start.22 = (bf16[16,32,128]{2,1,0:T(8,128)(2,1)S(1)}, bf16[16,32,128]{2,1,0:T(8,128)(2,1)S(1)}, u32[]{:S(2)}, u32[]{:S(2)}) collective-permute-start(bf16[16,32,128]{2,1,0:T(8,128)(2,1)S(1)} %get-tuple-element.45.refs_0_), channel_id=1, source_target_pairs={{0,4},{2,6},{4,0},{6,2},{8,12},{10,14},{12,8},{14,10},{16,20},{18,... | collective-permute-start | bytes 393224 | tf_op jit(solution)/shard_map/ppermute | solution.py:237
  62.2 10.2 %collective-permute-start.10 = (bf16[16,64,128]{2,1,0:T(8,128)(2,1)S(1)}, bf16[16,64,128]{2,1,0:T(8,128)(2,1)S(1)}, u32[]{:S(2)}, u32[]{:S(2)}) collective-permute-start(bf16[16,64,128]{2,1,0:T(8,128)(2,1)S(1)} %shard_map.77.refs_0_), channel_id=1, source_target_pairs={{0,2},{2,0},{4,6},{6,4},{8,10},{10,8},{12,14},{14,12},{16,18},{18,... | collective-permute-start | bytes 786440 | tf_op jit(solution)/shard_map/ppermute | solution.py:237
  62.5 9.9 %collective-permute-start.11 = (bf16[16,64,128]{2,1,0:T(8,128)(2,1)S(1)}, bf16[16,64,128]{2,1,0:T(8,128)(2,1)S(1)}, u32[]{:S(2)}, u32[]{:S(2)}) collective-permute-start(bf16[16,64,128]{2,1,0:T(8,128)(2,1)S(1)} %collective-permute-done.9.refs_1_), channel_id=1, source_target_pairs={{0,2},{2,0},{4,6},{6,4},{8,10},{10,8},{12,14},{14,12},{16,18},{18,... | collective-permute-start | bytes 786440 | tf_op jit(solution)/shard_map/ppermute | solution.py:237
  66.3 2.4 %collective-permute-start.28 = (bf16[16,32,128]{2,1,0:T(8,128)(2,1)S(1)}, bf16[16,32,128]{2,1,0:T(8,128)(2,1)S(1)}, u32[]{:S(2)}, u32[]{:S(2)}) collective-permute-start(bf16[16,32,128]{2,1,0:T(8,128)(2,1)S(1)} %collective-permute-done.26.refs_1_), channel_id=1, source_target_pairs={{0,2},{2,0},{4,6},{6,4},{8,10},{10,8},{12,14},{14,12},{16,18},{18,... | collective-permute-start | bytes 393224 | tf_op jit(solution)/shard_map/ppermute | solution.py:237
  66.3 4.6 %collective-permute-start.23 = (bf16[16,32,128]{2,1,0:T(8,128)(2,1)S(1)}, bf16[16,32,128]{2,1,0:T(8,128)(2,1)S(1)}, u32[]{:S(2)}, u32[]{:S(2)}) collective-permute-start(bf16[16,32,128]{2,1,0:T(8,128)(2,1)S(1)} %get-tuple-element.45.refs_0_), channel_id=1, source_target_pairs={{0,2},{2,0},{4,6},{6,4},{8,10},{10,8},{12,14},{14,12},{16,18},{18,... | collective-permute-start | bytes 393224 | tf_op jit(solution)/shard_map/ppermute | solution.py:237
  68.0 2.9 %collective-permute-start.24 = (bf16[16,32,128]{2,1,0:T(8,128)(2,1)S(1)}, bf16[16,32,128]{2,1,0:T(8,128)(2,1)S(1)}, u32[]{:S(2)}, u32[]{:S(2)}) collective-permute-start(bf16[16,32,128]{2,1,0:T(8,128)(2,1)S(1)} %collective-permute-done.22.refs_1_), channel_id=1, source_target_pairs={{0,2},{2,0},{4,6},{6,4},{8,10},{10,8},{12,14},{14,12},{16,18},{18,... | collective-permute-start | bytes 393224 | tf_op jit(solution)/shard_map/ppermute | solution.py:237
  69.4 4.5 %collective-permute-start.29 = (bf16[32,1024]{1,0:T(8,128)(2,1)S(1)}, bf16[32,1024]{1,0:T(8,128)(2,1)S(1)}, u32[]{:S(2)}, u32[]{:S(2)}) collective-permute-start(bf16[32,1024]{1,0:T(8,128)(2,1)S(1)} %shard_map.85), channel_id=1, source_target_pairs={{0,1},{1,0},{2,3},{3,2},{4,5},{5,4},{6,7},{7,6},{8,9},{9,8},{10,11... | collective-permute-start | bytes 196616 | tf_op jit(solution)/shard_map/ppermute | solution.py:240
  71.7 4.3 %collective-permute-start.25 = (bf16[32,1024]{1,0:T(8,128)(2,1)S(1)}, bf16[32,1024]{1,0:T(8,128)(2,1)S(1)}, u32[]{:S(2)}, u32[]{:S(2)}) collective-permute-start(bf16[32,1024]{1,0:T(8,128)(2,1)S(1)} %shard_map.84), channel_id=1, source_target_pairs={{0,1},{1,0},{2,3},{3,2},{4,5},{5,4},{6,7},{7,6},{8,9},{9,8},{10,11... | collective-permute-start | bytes 196616 | tf_op jit(solution)/shard_map/ppermute | solution.py:240
where the time goes:
time: 76.9 us; the launch traced here: 76.7 us
  waiting for transfers between devices  36.5 us (47%)
  starting transfers between devices  31.4 us (41%)
  Pallas kernels  6.66 us (9%)
  between operations  1.48 us (2%)
    ppermute x27, waiting for transfers between devices, move(): return lax.ppermute(value, 'row', digit_shift(sizes, which, by))  29.6 us
    ppermute x27, starting transfers between devices, move(): return lax.ppermute(value, 'row', digit_shift(sizes, which, by))  26.7 us
    ppermute x3, waiting for transfers between devices, across(): lax.ppermute(value, 'col', [(b, (b + by) % n_cols) for b in range(n_cols)])  6.88 us
    pallas_call x13, Pallas kernels, call(): pl.pallas_call(kernel, out_shape=tuple(outs), in_specs=[smem] * len(scala...  6.66 us
    ppermute x3, starting transfers between devices, across(): lax.ppermute(value, 'col', [(b, (b + by) % n_cols) for b in range(n_cols)])  4.71 us
  transfers between devices with their start and end apart: 30, of which 16 were waited for; matrix products, arithmetic and copies ran while one was open for 0% of the time, Pallas kernels for 5%

commit v1 on v0

--- a/solution.py
+++ b/solution.py
@@ -16,7 +16,6 @@
 SEND = jnp.float32
 SPARE = 1024 * 1024
 PLANS = 2
-CUTS = 2
 
 
 def slots_a_step(slots, rows, size):
@@ -164,14 +163,11 @@
     lax.fori_loop(0, refs[0].shape[0], step, 0, unroll=True if refs[0].shape[0] < 8 else 4)
 
 
-def join_kernel(cuts, *refs):
-    arrays, outs = refs[:-cuts], refs[-cuts:]
-    n = arrays[0].shape[0]
-    m = outs[0].shape[1]
-    for h, out in enumerate(outs):
-        for i, ref in enumerate(arrays):
-            for j in range(n):
-                out[i * n + j] = ref[j, h * m : (h + 1) * m]
+def join_kernel(*refs):
+    n = refs[0].shape[0]
+    for i, ref in enumerate(refs[:-1]):
+        for j in range(n):
+            refs[-1][i * n + j] = ref[j]
 
 
 def second_kernel(sizes, groups, pattern, count, *refs):
@@ -225,7 +221,6 @@
     columns_one = features * n_rows // n_cols // size
     columns_two = features // size
     groups = max(1, n_rows // columns_one)
-    cuts = CUTS if n_cols == 2 and groups == 1 else 1
     units = columns_one * groups
     per = units // (width * cores)
     each = per // depth
@@ -298,11 +293,10 @@
         arrays = [outs[0]] + [move(out, 0, k + 1) for k, out in enumerate(outs[1:])]
         return call(finish_kernel, [jax.ShapeDtypeStruct(arrays[0].shape, jnp.bfloat16)], [], arrays)[0]
 
-    def gather_depth(hidden, cuts):
+    def gather_depth(hidden):
         arrays = [hidden] + [move(hidden, 0, k) for k in range(1, depth)]
-        joined = (depth * each, hidden.shape[1] // cuts, hidden.shape[2])
-        outs = [jax.ShapeDtypeStruct(joined, jnp.bfloat16)] * cuts
-        return call(functools.partial(join_kernel, cuts), outs, [], arrays)
+        joined = (depth * each,) + hidden.shape[1:]
+        return call(join_kernel, [jax.ShapeDtypeStruct(joined, jnp.bfloat16)], [], arrays)[0]
 
     def gather_width(line):
         far = [move(line, 1, k) for k in range(1, width)]
@@ -334,24 +328,16 @@
         "reduce_core": reduce_core,
         "reduce_width": reduce_width,
         "reduce_depth": reduce_depth,
+        "gather_depth": gather_depth,
+        "gather_width": gather_width,
     }
     for run in stages.values():
         for name in chunks:
             chunks[name] = run(chunks[name])
-    lines = gather_depth(chunks["theirs"], cuts)
-    own_line = gather_depth(chunks["own"], 1)[0]
-    rest = []
-    for line in lines:
-        pieces = gather_width(line)
-        rest.append(second(pieces, plans, jnp.bfloat16))
-    pieces = gather_width(own_line)
-    mine = second(pieces, plans, jnp.float32)
+    rest = second(chunks["theirs"], plans, jnp.bfloat16)
+    mine = second(chunks["own"], plans, jnp.float32)
     for k in range(1, n_cols):
-        back = []
-        for part in rest:
-            rows = own_rows if cuts == 1 else part.shape[0]
-            back.append(across(lax.slice_in_dim(part, (k - 1) * rows, k * rows, axis=0), -k))
-        back = back[0] if cuts == 1 else jnp.concatenate(back, axis=0)
+        back = across(lax.slice_in_dim(rest, (k - 1) * own_rows, k * own_rows, axis=0), -k)
         mine = mine + back.astype(jnp.float32)
     return jnp.maximum(mine + bias_value, 0.0).astype(jnp.bfloat16)
 

time: 76.9 us -> 72.3 us (0.940)
  waiting for transfers between devices: 36.5 us -> 34.5 us
  starting transfers between devices: 31.4 us -> 29.6 us
    ppermute x3 -> x2, waiting for transfers between devices: 6.88 us -> 3.86 us  [across(): lax.ppermute(value, 'col', [(b, (b + by) % n_cols) for b in range(n_cols)])]
    ppermute x27 -> x24, starting transfers between devices: 26.7 us -> 25 us  [move(): return lax.ppermute(value, 'row', digit_shift(sizes, which, by))]
    ppermute x27 -> x24, waiting for transfers between devices: 29.6 us -> 30.6 us  [move(): return lax.ppermute(value, 'row', digit_shift(sizes, which, by))]
    pallas_call x13 -> x12, Pallas kernels: 6.66 us -> 5.94 us  [call(): pl.pallas_call(kernel, out_shape=tuple(outs), in_specs=[smem] * len(scala...]
    ppermute x3 -> x2, starting transfers between devices: 4.71 us -> 4.55 us  [across(): lax.ppermute(value, 'col', [(b, (b + by) % n_cols) for b in range(n_cols)])]
  transfers between devices with their start and end apart: 30 -> 26, of which waited for: 16 -> 14; matrix products, arithmetic and copies ran while one was open for 0% -> 0% of each run, Pallas kernels for 5% -> 7%
where the time goes in v1:
time: 72.3 us; the launch traced here: 72.2 us
  waiting for transfers between devices  34.5 us (48%)
  starting transfers between devices  29.6 us (41%)
  Pallas kernels  5.94 us (8%)
  between operations  1.44 us (2%)
    ppermute x24, waiting for transfers between devices, move(): return lax.ppermute(value, 'row', digit_shift(sizes, which, by))  30.6 us
    ppermute x24, starting transfers between devices, move(): return lax.ppermute(value, 'row', digit_shift(sizes, which, by))  25 us
    pallas_call x12, Pallas kernels, call(): pl.pallas_call(kernel, out_shape=tuple(outs), in_specs=[smem] * len(scala...  5.94 us
    ppermute x2, starting transfers between devices, across(): lax.ppermute(value, 'col', [(b, (b + by) % n_cols) for b in range(n_cols)])  4.55 us
    ppermute x2, waiting for transfers between devices, across(): lax.ppermute(value, 'col', [(b, (b + by) % n_cols) for b in range(n_cols)])  3.86 us
  transfers between devices with their start and end apart: 26, of which 14 were waited for; matrix products, arithmetic and copies ran while one was open for 0% of the time, Pallas kernels for 7%

profile of v1, /device:TPU:0, one launch (start us, length us, event | category | flops | bytes accessed | tf_op | source)
XLA Modules:
  0.0 72.2 jit_solution(2172636478042236536)
XLA Ops:
  0.0 3.0 %collective-permute-start.12 = (bf16[64,1024]{1,0:T(8,128)(2,1)}, bf16[64,1024]{1,0:T(8,128)(2,1)S(1)}, u32[]{:S(2)}, u32[]{:S(2)}) collective-permute-start(bf16[64,1024]{1,0:T(8,128)(2,1)} %refs_3_.1), channel_id=1, source_target_pairs={{0,1},{1,0},{2,3},{3,2},{4,5},{5,4},{6,7},{7,6},{8,9},{9,8},{10,11... | collective-permute-start | bytes 393224 | tf_op jit(solution)/shard_map/ppermute | solution.py:235
  3.6 2.7 %shard_map.73 = (f32[16,64,128]{2,1,0:T(8,128)S(1)}, f32[16,64,128]{2,1,0:T(8,128)S(1)}, f32[16,64,128]{2,1,0:T(8,128)S(1)}, f32[16,64,128]{2,1,0:T(8,128)S(1)},...) custom-call(s32[1,1]{1,0:T(1,128)S(6)} %copy.8.refs_0_.refs_1_, s32[1,64]{1,0:T(1,128)} %bitcast.19, ...), custom_call_target="tpu_custom_call" | custom-call | flops 134217728 | bytes 2097152 | tf_op jit(solution)/shard_map/pallas_call | solution.py:244
  6.7 1.1 %shard_map.79 = (f32[16,64,128]{2,1,0:T(8,128)S(1)}, f32[16,64,128]{2,1,0:T(8,128)S(1)}, f32[16,64,128]{2,1,0:T(8,128)S(1)}, f32[16,64,128]{2,1,0:T(8,128)S(1)}) custom-call(s32[1,64]{1,0:T(1,128)S(4)} %get-tuple-element.33.refs_0_, s32[1,1]{1,0:T(1,128)S(6)} %copy.8.refs_0_.refs_1_, bf16[64,1024]{1,0:T(8,128)(2,1)S(1)} %collective-permute-done.12.refs_2_, ...), custom_call_target="tpu_custom_call" | custom-call | flops 134217728 | bytes 2097152 | tf_op jit(solution)/shard_map/pallas_call | solution.py:244
  8.9 0.9 %collective-permute-done.14.right = f32[16,64,128]{2,1,0:T(8,128)S(1)} collective-permute-done((f32[16,64,128]{2,1,0:T(8,128)S(1)}, f32[16,64,128]{2,1,0:T(8,128)S(1)}, u32[]{:S(2)}, u32[]{:S(2)}) %collective-permute-start.14) | collective-permute-done | bytes 524320 | tf_op jit(solution)/shard_map/ppermute | solution.py:232
  9.8 1.8 %collective-permute-start.15 = (bf16[16,64,128]{2,1,0:T(8,128)(2,1)S(1)}, bf16[16,64,128]{2,1,0:T(8,128)(2,1)S(1)}, u32[]{:S(2)}, u32[]{:S(2)}) collective-permute-start(bf16[16,64,128]{2,1,0:T(8,128)(2,1)S(1)} %shard_map.80), channel_id=1, source_target_pairs={{0,4},{2,6},{4,0},{6,2},{8,12},{10,14},{12,8},{14,10},{16,20},{18,... | collective-permute-start | bytes 786440 | tf_op jit(solution)/shard_map/ppermute | solution.py:232
  11.7 0.7 collective-permute-start.2
  12.3 6.7 %collective-permute-done.15 = bf16[16,64,128]{2,1,0:T(8,128)(2,1)S(1)} collective-permute-done((bf16[16,64,128]{2,1,0:T(8,128)(2,1)S(1)}, bf16[16,64,128]{2,1,0:T(8,128)(2,1)S(1)}, u32[]{:S(2)}, u32[]{:S(2)}) %collective-permute-start.15) | collective-permute-done | bytes 262176 | tf_op jit(solution)/shard_map/ppermute | solution.py:232
  19.2 1.9 %collective-permute-start.16 = (bf16[4,64,128]{2,1,0:T(8,128)(2,1)S(1)}, bf16[4,64,128]{2,1,0:T(8,128)(2,1)S(1)}, u32[]{:S(2)}, u32[]{:S(2)}) collective-permute-start(bf16[4,64,128]{2,1,0:T(8,128)(2,1)S(1)} %get-tuple-element.40), channel_id=1, source_target_pairs={{0,8},{2,10},{4,12},{6,14},{8,0},{10,2},{12,4},{14,6},{16,24},{18,... | collective-permute-start | bytes 196616 | tf_op jit(solution)/shard_map/ppermute | solution.py:232
  21.0 2.6 %collective-permute-start.17 = (bf16[4,64,128]{2,1,0:T(8,128)(2,1)S(1)}, bf16[4,64,128]{2,1,0:T(8,128)(2,1)S(1)}, u32[]{:S(2)}, u32[]{:S(2)}) collective-permute-start(bf16[4,64,128]{2,1,0:T(8,128)(2,1)S(1)} %get-tuple-element.41), channel_id=1, source_target_pairs={{0,16},{2,18},{4,20},{6,22},{8,24},{10,26},{12,28},{14,30},{16,0},... | collective-permute-start | bytes 196616 | tf_op jit(solution)/shard_map/ppermute | solution.py:232
  24.0 3.6 %collective-permute-done.17.refs_2_ = bf16[4,64,128]{2,1,0:T(8,128)(2,1)S(1)} collective-permute-done((bf16[4,64,128]{2,1,0:T(8,128)(2,1)S(1)}, bf16[4,64,128]{2,1,0:T(8,128)(2,1)S(1)}, u32[]{:S(2)}, u32[]{:S(2)}) %collective-permute-start.17) | collective-permute-done | bytes 65568 | tf_op jit(solution)/shard_map/ppermute | solution.py:232
  27.6 2.7 %collective-permute-done.18.refs_3_ = bf16[4,64,128]{2,1,0:T(8,128)(2,1)S(1)} collective-permute-done((bf16[4,64,128]{2,1,0:T(8,128)(2,1)S(1)}, bf16[4,64,128]{2,1,0:T(8,128)(2,1)S(1)}, u32[]{:S(2)}, u32[]{:S(2)}) %collective-permute-start.18) | collective-permute-done | bytes 65568 | tf_op jit(solution)/shard_map/ppermute | solution.py:232
  30.4 0.7 %collective-permute-start.20 = (bf16[4,64,128]{2,1,0:T(8,128)(2,1)S(1)}, bf16[4,64,128]{2,1,0:T(8,128)(2,1)S(1)}, u32[]{:S(2)}, u32[]{:S(2)}) collective-permute-start(bf16[4,64,128]{2,1,0:T(8,128)(2,1)S(1)} %shard_map.82.refs_0_), channel_id=1, source_target_pairs={{0,16},{2,18},{4,20},{6,22},{8,24},{10,26},{12,28},{14,30},{16,0},... | collective-permute-start | bytes 196616 | tf_op jit(solution)/shard_map/ppermute | solution.py:232
  31.1 3.6 %collective-permute-start.21 = (bf16[4,64,128]{2,1,0:T(8,128)(2,1)S(1)}, bf16[4,64,128]{2,1,0:T(8,128)(2,1)S(1)}, u32[]{:S(2)}, u32[]{:S(2)}) collective-permute-start(bf16[4,64,128]{2,1,0:T(8,128)(2,1)S(1)} %shard_map.82.refs_0_), channel_id=1, source_target_pairs={{0,24},{2,26},{4,28},{6,30},{8,16},{10,18},{12,20},{14,22},{16,8},... | collective-permute-start | bytes 196616 | tf_op jit(solution)/shard_map/ppermute | solution.py:232
  34.8 0.9 %collective-permute-done.20.refs_2_ = bf16[4,64,128]{2,1,0:T(8,128)(2,1)S(1)} collective-permute-done((bf16[4,64,128]{2,1,0:T(8,128)(2,1)S(1)}, bf16[4,64,128]{2,1,0:T(8,128)(2,1)S(1)}, u32[]{:S(2)}, u32[]{:S(2)}) %collective-permute-start.20) | collective-permute-done | bytes 65568 | tf_op jit(solution)/shard_map/ppermute | solution.py:232
  35.6 2.2 %collective-permute-done.21.refs_3_ = bf16[4,64,128]{2,1,0:T(8,128)(2,1)S(1)} collective-permute-done((bf16[4,64,128]{2,1,0:T(8,128)(2,1)S(1)}, bf16[4,64,128]{2,1,0:T(8,128)(2,1)S(1)}, u32[]{:S(2)}, u32[]{:S(2)}) %collective-permute-start.21) | collective-permute-done | bytes 65568 | tf_op jit(solution)/shard_map/ppermute | solution.py:232
  37.8 1.6 %collective-permute-start.22 = (bf16[16,64,128]{2,1,0:T(8,128)(2,1)S(1)}, bf16[16,64,128]{2,1,0:T(8,128)(2,1)S(1)}, u32[]{:S(2)}, u32[]{:S(2)}) collective-permute-start(bf16[16,64,128]{2,1,0:T(8,128)(2,1)S(1)} %shard_map.83.refs_0_), channel_id=1, source_target_pairs={{0,4},{2,6},{4,0},{6,2},{8,12},{10,14},{12,8},{14,10},{16,20},{18,... | collective-permute-start | bytes 786440 | tf_op jit(solution)/shard_map/ppermute | solution.py:232
  39.6 3.6 %collective-permute-start.4 = (bf16[4,64,128]{2,1,0:T(8,128)(2,1)S(1)}, bf16[4,64,128]{2,1,0:T(8,128)(2,1)S(1)}, u32[]{:S(2)}, u32[]{:S(2)}) collective-permute-start(bf16[4,64,128]{2,1,0:T(8,128)(2,1)S(1)} %get-tuple-element.31), channel_id=1, source_target_pairs={{0,16},{2,18},{4,20},{6,22},{8,24},{10,26},{12,28},{14,30},{16,0},... | collective-permute-start | bytes 196616 | tf_op jit(solution)/shard_map/ppermute | solution.py:232
  43.2 0.8 %collective-permute-start.5 = (bf16[4,64,128]{2,1,0:T(8,128)(2,1)S(1)}, bf16[4,64,128]{2,1,0:T(8,128)(2,1)S(1)}, u32[]{:S(2)}, u32[]{:S(2)}) collective-permute-start(bf16[4,64,128]{2,1,0:T(8,128)(2,1)S(1)} %get-tuple-element.32), channel_id=1, source_target_pairs={{0,24},{2,26},{4,28},{6,30},{8,16},{10,18},{12,20},{14,22},{16,8},... | collective-permute-start | bytes 196616 | tf_op jit(solution)/shard_map/ppermute | solution.py:232
  44.0 1.8 %collective-permute-done.4.refs_2_ = bf16[4,64,128]{2,1,0:T(8,128)(2,1)S(1)} collective-permute-done((bf16[4,64,128]{2,1,0:T(8,128)(2,1)S(1)}, bf16[4,64,128]{2,1,0:T(8,128)(2,1)S(1)}, u32[]{:S(2)}, u32[]{:S(2)}) %collective-permute-start.4) | collective-permute-done | bytes 65568 | tf_op jit(solution)/shard_map/ppermute | solution.py:232
  45.7 3.9 %collective-permute-done.5.refs_3_ = bf16[4,64,128]{2,1,0:T(8,128)(2,1)S(1)} collective-permute-done((bf16[4,64,128]{2,1,0:T(8,128)(2,1)S(1)}, bf16[4,64,128]{2,1,0:T(8,128)(2,1)S(1)}, u32[]{:S(2)}, u32[]{:S(2)}) %collective-permute-start.5) | collective-permute-done | bytes 65568 | tf_op jit(solution)/shard_map/ppermute | solution.py:232
  49.7 1.0 %collective-permute-start.6 = (bf16[4,64,128]{2,1,0:T(8,128)(2,1)S(1)}, bf16[4,64,128]{2,1,0:T(8,128)(2,1)S(1)}, u32[]{:S(2)}, u32[]{:S(2)}) collective-permute-start(bf16[4,64,128]{2,1,0:T(8,128)(2,1)S(1)} %shard_map.76.refs_0_), channel_id=1, source_target_pairs={{0,8},{2,10},{4,12},{6,14},{8,0},{10,2},{12,4},{14,6},{16,24},{18,... | collective-permute-start | bytes 196616 | tf_op jit(solution)/shard_map/ppermute | solution.py:232
  50.7 0.7 %collective-permute-start.7 = (bf16[4,64,128]{2,1,0:T(8,128)(2,1)S(1)}, bf16[4,64,128]{2,1,0:T(8,128)(2,1)S(1)}, u32[]{:S(2)}, u32[]{:S(2)}) collective-permute-start(bf16[4,64,128]{2,1,0:T(8,128)(2,1)S(1)} %shard_map.76.refs_0_), channel_id=1, source_target_pairs={{0,16},{2,18},{4,20},{6,22},{8,24},{10,26},{12,28},{14,30},{16,0},... | collective-permute-start | bytes 196616 | tf_op jit(solution)/shard_map/ppermute | solution.py:232
  51.4 2.7 %collective-permute-start.8 = (bf16[4,64,128]{2,1,0:T(8,128)(2,1)S(1)}, bf16[4,64,128]{2,1,0:T(8,128)(2,1)S(1)}, u32[]{:S(2)}, u32[]{:S(2)}) collective-permute-start(bf16[4,64,128]{2,1,0:T(8,128)(2,1)S(1)} %shard_map.76.refs_0_), channel_id=1, source_target_pairs={{0,24},{2,26},{4,28},{6,30},{8,16},{10,18},{12,20},{14,22},{16,8},... | collective-permute-start | bytes 196616 | tf_op jit(solution)/shard_map/ppermute | solution.py:232
  54.2 2.4 %collective-permute-done.7.refs_2_ = bf16[4,64,128]{2,1,0:T(8,128)(2,1)S(1)} collective-permute-done((bf16[4,64,128]{2,1,0:T(8,128)(2,1)S(1)}, bf16[4,64,128]{2,1,0:T(8,128)(2,1)S(1)}, u32[]{:S(2)}, u32[]{:S(2)}) %collective-permute-start.7) | collective-permute-done | bytes 65568 | tf_op jit(solution)/shard_map/ppermute | solution.py:232
  56.5 0.9 %collective-permute-done.8.refs_3_ = bf16[4,64,128]{2,1,0:T(8,128)(2,1)S(1)} collective-permute-done((bf16[4,64,128]{2,1,0:T(8,128)(2,1)S(1)}, bf16[4,64,128]{2,1,0:T(8,128)(2,1)S(1)}, u32[]{:S(2)}, u32[]{:S(2)}) %collective-permute-start.8) | collective-permute-done | bytes 65568 | tf_op jit(solution)/shard_map/ppermute | solution.py:232
  57.5 1.6 %collective-permute-start.9 = (bf16[16,64,128]{2,1,0:T(8,128)(2,1)S(1)}, bf16[16,64,128]{2,1,0:T(8,128)(2,1)S(1)}, u32[]{:S(2)}, u32[]{:S(2)}) collective-permute-start(bf16[16,64,128]{2,1,0:T(8,128)(2,1)S(1)} %shard_map.77.refs_0_), channel_id=1, source_target_pairs={{0,4},{2,6},{4,0},{6,2},{8,12},{10,14},{12,8},{14,10},{16,20},{18,... | collective-permute-start | bytes 786440 | tf_op jit(solution)/shard_map/ppermute | solution.py:232
  59.6 4.3 %collective-permute-done.9.refs_1_ = bf16[16,64,128]{2,1,0:T(8,128)(2,1)S(1)} collective-permute-done((bf16[16,64,128]{2,1,0:T(8,128)(2,1)S(1)}, bf16[16,64,128]{2,1,0:T(8,128)(2,1)S(1)}, u32[]{:S(2)}, u32[]{:S(2)}) %collective-permute-start.9) | collective-permute-done | bytes 262176 | tf_op jit(solution)/shard_map/ppermute | solution.py:232
  64.6 0.9 %shard_map.84 = bf16[64,1024]{1,0:T(8,128)(2,1)S(1)} custom-call(s32[1,64]{1,0:T(1,128)S(4)} %get-tuple-element.24.pattern, s32[1,1]{1,0:T(1,128)S(6)} %copy.9.count, bf16[16,64,128]{2,1,0:T(8,128)(2,1)S(1)} %shard_map.83.refs_0_, bf16[16,64,128]{2,1,0:T(8,128)(2,1)S(1)} %collective-permute-done.22.refs_1_, ...), custom_call_target="tpu_custom_call" | custom-call | flops 134217728 | bytes 2097152 | tf_op jit(solution)/shard_map/pallas_call | solution.py:244
  65.5 1.6 %collective-permute-start.25 = (bf16[64,1024]{1,0:T(8,128)(2,1)S(1)}, bf16[64,1024]{1,0:T(8,128)(2,1)S(1)}, u32[]{:S(2)}, u32[]{:S(2)}) collective-permute-start(bf16[64,1024]{1,0:T(8,128)(2,1)S(1)} %shard_map.84), channel_id=1, source_target_pairs={{0,1},{1,0},{2,3},{3,2},{4,5},{5,4},{6,7},{7,6},{8,9},{9,8},{10,11... | collective-permute-start | bytes 393224 | tf_op jit(solution)/shard_map/ppermute | solution.py:235
  67.1 0.9 %shard_map.78 = f32[64,1024]{1,0:T(8,128)S(1)} custom-call(s32[1,64]{1,0:T(1,128)S(4)} %get-tuple-element.24.pattern, s32[1,1]{1,0:T(1,128)S(6)} %copy.9.count, bf16[16,64,128]{2,1,0:T(8,128)(2,1)S(1)} %shard_map.77.refs_0_, bf16[16,64,128]{2,1,0:T(8,128)(2,1)S(1)} %collective-permute-done.9.refs_1_, ...), custom_call_target="tpu_custom_call" | custom-call | tf_op jit(solution)/shard_map/pallas_call | solution.py:244
  67.9 3.5 %collective-permute-done.25 = bf16[64,1024]{1,0:T(8,128)(2,1)S(1)} collective-permute-done((bf16[64,1024]{1,0:T(8,128)(2,1)S(1)}, bf16[64,1024]{1,0:T(8,128)(2,1)S(1)}, u32[]{:S(2)}, u32[]{:S(2)}) %collective-permute-start.25) | collective-permute-done | bytes 131104 | tf_op jit(solution)/shard_map/ppermute | solution.py:235
  71.5 0.7 maximum_convert_fusion
  (35 shorter events, 2.9 us)
Async XLA Ops:
  0.0 6.7 %collective-permute-start.12 = (bf16[64,1024]{1,0:T(8,128)(2,1)}, bf16[64,1024]{1,0:T(8,128)(2,1)S(1)}, u32[]{:S(2)}, u32[]{:S(2)}) collective-permute-start(bf16[64,1024]{1,0:T(8,128)(2,1)} %refs_3_.1), channel_id=1, source_target_pairs={{0,1},{1,0},{2,3},{3,2},{4,5},{5,4},{6,7},{7,6},{8,9},{9,8},{10,11... | collective-permute-start | bytes 393224 | tf_op jit(solution)/shard_map/ppermute | solution.py:235
  7.8 2.0 %collective-permute-start.14 = (f32[16,64,128]{2,1,0:T(8,128)S(1)}, f32[16,64,128]{2,1,0:T(8,128)S(1)}, u32[]{:S(2)}, u32[]{:S(2)}) collective-permute-start(f32[16,64,128]{2,1,0:T(8,128)S(1)} %get-tuple-element.38), channel_id=1, source_target_pairs={{0,2},{2,0},{4,6},{6,4},{8,10},{10,8},{12,14},{14,12},{16,18},{18,... | collective-permute-start | bytes 1572872 | tf_op jit(solution)/shard_map/ppermute | solution.py:232
  7.9 3.7 %collective-permute-start.1 = (f32[16,64,128]{2,1,0:T(8,128)S(1)}, f32[16,64,128]{2,1,0:T(8,128)S(1)}, u32[]{:S(2)}, u32[]{:S(2)}) collective-permute-start(f32[16,64,128]{2,1,0:T(8,128)S(1)} %get-tuple-element.28), channel_id=1, source_target_pairs={{0,2},{2,0},{4,6},{6,4},{8,10},{10,8},{12,14},{14,12},{16,18},{18,... | collective-permute-start | bytes 1572872 | tf_op jit(solution)/shard_map/ppermute | solution.py:232
  8.4 4.0 %collective-permute-start.13 = (f32[16,64,128]{2,1,0:T(8,128)S(1)}, f32[16,64,128]{2,1,0:T(8,128)S(1)}, u32[]{:S(2)}, u32[]{:S(2)}) collective-permute-start(f32[16,64,128]{2,1,0:T(8,128)S(1)} %get-tuple-element.36), channel_id=1, source_target_pairs={{0,2},{2,0},{4,6},{6,4},{8,10},{10,8},{12,14},{14,12},{16,18},{18,... | collective-permute-start | bytes 1572872 | tf_op jit(solution)/shard_map/ppermute | solution.py:232
  8.4 30.9 %collective-permute-start = (f32[16,64,128]{2,1,0:T(8,128)S(1)}, f32[16,64,128]{2,1,0:T(8,128)S(1)}, u32[]{:S(2)}, u32[]{:S(2)}) collective-permute-start(f32[16,64,128]{2,1,0:T(8,128)S(1)} %get-tuple-element.26), channel_id=1, source_target_pairs={{0,2},{2,0},{4,6},{6,4},{8,10},{10,8},{12,14},{14,12},{16,18},{18,... | collective-permute-start | bytes 1572872 | tf_op jit(solution)/shard_map/ppermute | solution.py:232
  9.8 9.2 %collective-permute-start.15 = (bf16[16,64,128]{2,1,0:T(8,128)(2,1)S(1)}, bf16[16,64,128]{2,1,0:T(8,128)(2,1)S(1)}, u32[]{:S(2)}, u32[]{:S(2)}) collective-permute-start(bf16[16,64,128]{2,1,0:T(8,128)(2,1)S(1)} %shard_map.80), channel_id=1, source_target_pairs={{0,4},{2,6},{4,0},{6,2},{8,12},{10,14},{12,8},{14,10},{16,20},{18,... | collective-permute-start | bytes 786440 | tf_op jit(solution)/shard_map/ppermute | solution.py:232
  11.7 27.7 %collective-permute-start.2 = (bf16[16,64,128]{2,1,0:T(8,128)(2,1)S(1)}, bf16[16,64,128]{2,1,0:T(8,128)(2,1)S(1)}, u32[]{:S(2)}, u32[]{:S(2)}) collective-permute-start(bf16[16,64,128]{2,1,0:T(8,128)(2,1)S(1)} %shard_map.74), channel_id=1, source_target_pairs={{0,4},{2,6},{4,0},{6,2},{8,12},{10,14},{12,8},{14,10},{16,20},{18,... | collective-permute-start | bytes 786440 | tf_op jit(solution)/shard_map/ppermute | solution.py:232
  19.1 45.6 %copy-start = (bf16[1,1,64,128,128]{4,3,2,1,0:T(8,128)(2,1)S(1)}, bf16[1,1,64,128,128]{4,3,2,1,0:T(8,128)(2,1)}, u32[]{:S(2)}) copy-start(bf16[1,1,64,128,128]{4,3,2,1,0:T(8,128)(2,1)} %param.11) | copy-start | bytes 6291460
  19.2 4.9 %collective-permute-start.16 = (bf16[4,64,128]{2,1,0:T(8,128)(2,1)S(1)}, bf16[4,64,128]{2,1,0:T(8,128)(2,1)S(1)}, u32[]{:S(2)}, u32[]{:S(2)}) collective-permute-start(bf16[4,64,128]{2,1,0:T(8,128)(2,1)S(1)} %get-tuple-element.40), channel_id=1, source_target_pairs={{0,8},{2,10},{4,12},{6,14},{8,0},{10,2},{12,4},{14,6},{16,24},{18,... | collective-permute-start | bytes 196616 | tf_op jit(solution)/shard_map/ppermute | solution.py:232
  21.0 6.6 %collective-permute-start.17 = (bf16[4,64,128]{2,1,0:T(8,128)(2,1)S(1)}, bf16[4,64,128]{2,1,0:T(8,128)(2,1)S(1)}, u32[]{:S(2)}, u32[]{:S(2)}) collective-permute-start(bf16[4,64,128]{2,1,0:T(8,128)(2,1)S(1)} %get-tuple-element.41), channel_id=1, source_target_pairs={{0,16},{2,18},{4,20},{6,22},{8,24},{10,26},{12,28},{14,30},{16,0},... | collective-permute-start | bytes 196616 | tf_op jit(solution)/shard_map/ppermute | solution.py:232
  23.6 6.7 %collective-permute-start.18 = (bf16[4,64,128]{2,1,0:T(8,128)(2,1)S(1)}, bf16[4,64,128]{2,1,0:T(8,128)(2,1)S(1)}, u32[]{:S(2)}, u32[]{:S(2)}) collective-permute-start(bf16[4,64,128]{2,1,0:T(8,128)(2,1)S(1)} %get-tuple-element.42), channel_id=1, source_target_pairs={{0,24},{2,26},{4,28},{6,30},{8,16},{10,18},{12,20},{14,22},{16,8},... | collective-permute-start | bytes 196616 | tf_op jit(solution)/shard_map/ppermute | solution.py:232
  30.3 4.5 %collective-permute-start.19 = (bf16[4,64,128]{2,1,0:T(8,128)(2,1)S(1)}, bf16[4,64,128]{2,1,0:T(8,128)(2,1)S(1)}, u32[]{:S(2)}, u32[]{:S(2)}) collective-permute-start(bf16[4,64,128]{2,1,0:T(8,128)(2,1)S(1)} %shard_map.82.refs_0_), channel_id=1, source_target_pairs={{0,8},{2,10},{4,12},{6,14},{8,0},{10,2},{12,4},{14,6},{16,24},{18,... | collective-permute-start | bytes 196616 | tf_op jit(solution)/shard_map/ppermute | solution.py:232
  30.4 5.2 %collective-permute-start.20 = (bf16[4,64,128]{2,1,0:T(8,128)(2,1)S(1)}, bf16[4,64,128]{2,1,0:T(8,128)(2,1)S(1)}, u32[]{:S(2)}, u32[]{:S(2)}) collective-permute-start(bf16[4,64,128]{2,1,0:T(8,128)(2,1)S(1)} %shard_map.82.refs_0_), channel_id=1, source_target_pairs={{0,16},{2,18},{4,20},{6,22},{8,24},{10,26},{12,28},{14,30},{16,0},... | collective-permute-start | bytes 196616 | tf_op jit(solution)/shard_map/ppermute | solution.py:232
  31.1 6.6 %collective-permute-start.21 = (bf16[4,64,128]{2,1,0:T(8,128)(2,1)S(1)}, bf16[4,64,128]{2,1,0:T(8,128)(2,1)S(1)}, u32[]{:S(2)}, u32[]{:S(2)}) collective-permute-start(bf16[4,64,128]{2,1,0:T(8,128)(2,1)S(1)} %shard_map.82.refs_0_), channel_id=1, source_target_pairs={{0,24},{2,26},{4,28},{6,30},{8,16},{10,18},{12,20},{14,22},{16,8},... | collective-permute-start | bytes 196616 | tf_op jit(solution)/shard_map/ppermute | solution.py:232
  37.8 21.3 %collective-permute-start.22 = (bf16[16,64,128]{2,1,0:T(8,128)(2,1)S(1)}, bf16[16,64,128]{2,1,0:T(8,128)(2,1)S(1)}, u32[]{:S(2)}, u32[]{:S(2)}) collective-permute-start(bf16[16,64,128]{2,1,0:T(8,128)(2,1)S(1)} %shard_map.83.refs_0_), channel_id=1, source_target_pairs={{0,4},{2,6},{4,0},{6,2},{8,12},{10,14},{12,8},{14,10},{16,20},{18,... | collective-permute-start | bytes 786440 | tf_op jit(solution)/shard_map/ppermute | solution.py:232
  39.5 4.5 %collective-permute-start.3 = (bf16[4,64,128]{2,1,0:T(8,128)(2,1)S(1)}, bf16[4,64,128]{2,1,0:T(8,128)(2,1)S(1)}, u32[]{:S(2)}, u32[]{:S(2)}) collective-permute-start(bf16[4,64,128]{2,1,0:T(8,128)(2,1)S(1)} %get-tuple-element.30), channel_id=1, source_target_pairs={{0,8},{2,10},{4,12},{6,14},{8,0},{10,2},{12,4},{14,6},{16,24},{18,... | collective-permute-start | bytes 196616 | tf_op jit(solution)/shard_map/ppermute | solution.py:232
  39.6 6.2 %collective-permute-start.4 = (bf16[4,64,128]{2,1,0:T(8,128)(2,1)S(1)}, bf16[4,64,128]{2,1,0:T(8,128)(2,1)S(1)}, u32[]{:S(2)}, u32[]{:S(2)}) collective-permute-start(bf16[4,64,128]{2,1,0:T(8,128)(2,1)S(1)} %get-tuple-element.31), channel_id=1, source_target_pairs={{0,16},{2,18},{4,20},{6,22},{8,24},{10,26},{12,28},{14,30},{16,0},... | collective-permute-start | bytes 196616 | tf_op jit(solution)/shard_map/ppermute | solution.py:232
  43.2 6.5 %collective-permute-start.5 = (bf16[4,64,128]{2,1,0:T(8,128)(2,1)S(1)}, bf16[4,64,128]{2,1,0:T(8,128)(2,1)S(1)}, u32[]{:S(2)}, u32[]{:S(2)}) collective-permute-start(bf16[4,64,128]{2,1,0:T(8,128)(2,1)S(1)} %get-tuple-element.32), channel_id=1, source_target_pairs={{0,24},{2,26},{4,28},{6,30},{8,16},{10,18},{12,20},{14,22},{16,8},... | collective-permute-start | bytes 196616 | tf_op jit(solution)/shard_map/ppermute | solution.py:232
  49.7 4.5 %collective-permute-start.6 = (bf16[4,64,128]{2,1,0:T(8,128)(2,1)S(1)}, bf16[4,64,128]{2,1,0:T(8,128)(2,1)S(1)}, u32[]{:S(2)}, u32[]{:S(2)}) collective-permute-start(bf16[4,64,128]{2,1,0:T(8,128)(2,1)S(1)} %shard_map.76.refs_0_), channel_id=1, source_target_pairs={{0,8},{2,10},{4,12},{6,14},{8,0},{10,2},{12,4},{14,6},{16,24},{18,... | collective-permute-start | bytes 196616 | tf_op jit(solution)/shard_map/ppermute | solution.py:232
  50.7 5.9 %collective-permute-start.7 = (bf16[4,64,128]{2,1,0:T(8,128)(2,1)S(1)}, bf16[4,64,128]{2,1,0:T(8,128)(2,1)S(1)}, u32[]{:S(2)}, u32[]{:S(2)}) collective-permute-start(bf16[4,64,128]{2,1,0:T(8,128)(2,1)S(1)} %shard_map.76.refs_0_), channel_id=1, source_target_pairs={{0,16},{2,18},{4,20},{6,22},{8,24},{10,26},{12,28},{14,30},{16,0},... | collective-permute-start | bytes 196616 | tf_op jit(solution)/shard_map/ppermute | solution.py:232
  51.4 6.1 %collective-permute-start.8 = (bf16[4,64,128]{2,1,0:T(8,128)(2,1)S(1)}, bf16[4,64,128]{2,1,0:T(8,128)(2,1)S(1)}, u32[]{:S(2)}, u32[]{:S(2)}) collective-permute-start(bf16[4,64,128]{2,1,0:T(8,128)(2,1)S(1)} %shard_map.76.refs_0_), channel_id=1, source_target_pairs={{0,24},{2,26},{4,28},{6,30},{8,16},{10,18},{12,20},{14,22},{16,8},... | collective-permute-start | bytes 196616 | tf_op jit(solution)/shard_map/ppermute | solution.py:232
  57.5 6.4 %collective-permute-start.9 = (bf16[16,64,128]{2,1,0:T(8,128)(2,1)S(1)}, bf16[16,64,128]{2,1,0:T(8,128)(2,1)S(1)}, u32[]{:S(2)}, u32[]{:S(2)}) collective-permute-start(bf16[16,64,128]{2,1,0:T(8,128)(2,1)S(1)} %shard_map.77.refs_0_), channel_id=1, source_target_pairs={{0,4},{2,6},{4,0},{6,2},{8,12},{10,14},{12,8},{14,10},{16,20},{18,... | collective-permute-start | bytes 786440 | tf_op jit(solution)/shard_map/ppermute | solution.py:232
  59.1 5.5 %collective-permute-start.23 = (bf16[16,64,128]{2,1,0:T(8,128)(2,1)S(1)}, bf16[16,64,128]{2,1,0:T(8,128)(2,1)S(1)}, u32[]{:S(2)}, u32[]{:S(2)}) collective-permute-start(bf16[16,64,128]{2,1,0:T(8,128)(2,1)S(1)} %shard_map.83.refs_0_), channel_id=1, source_target_pairs={{0,2},{2,0},{4,6},{6,4},{8,10},{10,8},{12,14},{14,12},{16,18},{18,... | collective-permute-start | bytes 786440 | tf_op jit(solution)/shard_map/ppermute | solution.py:232
  59.1 5.5 %collective-permute-start.24 = (bf16[16,64,128]{2,1,0:T(8,128)(2,1)S(1)}, bf16[16,64,128]{2,1,0:T(8,128)(2,1)S(1)}, u32[]{:S(2)}, u32[]{:S(2)}) collective-permute-start(bf16[16,64,128]{2,1,0:T(8,128)(2,1)S(1)} %collective-permute-done.22.refs_1_), channel_id=1, source_target_pairs={{0,2},{2,0},{4,6},{6,4},{8,10},{10,8},{12,14},{14,12},{16,18},{18,... | collective-permute-start | bytes 786440 | tf_op jit(solution)/shard_map/ppermute | solution.py:232
  59.6 7.4 %collective-permute-start.10 = (bf16[16,64,128]{2,1,0:T(8,128)(2,1)S(1)}, bf16[16,64,128]{2,1,0:T(8,128)(2,1)S(1)}, u32[]{:S(2)}, u32[]{:S(2)}) collective-permute-start(bf16[16,64,128]{2,1,0:T(8,128)(2,1)S(1)} %shard_map.77.refs_0_), channel_id=1, source_target_pairs={{0,2},{2,0},{4,6},{6,4},{8,10},{10,8},{12,14},{14,12},{16,18},{18,... | collective-permute-start | bytes 786440 | tf_op jit(solution)/shard_map/ppermute | solution.py:232
  63.9 3.1 %collective-permute-start.11 = (bf16[16,64,128]{2,1,0:T(8,128)(2,1)S(1)}, bf16[16,64,128]{2,1,0:T(8,128)(2,1)S(1)}, u32[]{:S(2)}, u32[]{:S(2)}) collective-permute-start(bf16[16,64,128]{2,1,0:T(8,128)(2,1)S(1)} %collective-permute-done.9.refs_1_), channel_id=1, source_target_pairs={{0,2},{2,0},{4,6},{6,4},{8,10},{10,8},{12,14},{14,12},{16,18},{18,... | collective-permute-start | bytes 786440 | tf_op jit(solution)/shard_map/ppermute | solution.py:232
  65.5 6.0 %collective-permute-start.25 = (bf16[64,1024]{1,0:T(8,128)(2,1)S(1)}, bf16[64,1024]{1,0:T(8,128)(2,1)S(1)}, u32[]{:S(2)}, u32[]{:S(2)}) collective-permute-start(bf16[64,1024]{1,0:T(8,128)(2,1)S(1)} %shard_map.84), channel_id=1, source_target_pairs={{0,1},{1,0},{2,3},{3,2},{4,5},{5,4},{6,7},{7,6},{8,9},{9,8},{10,11... | collective-permute-start | bytes 393224 | tf_op jit(solution)/shard_map/ppermute | solution.py:235
